TPU v7x, 32 devices: a whole 2x2x4 slice. The times are simulated.
32 devices in a mesh: sweep: 4 (over z), layer: 8 (over y, x, core).
Axes of the slice: x: 2, y: 2, z: 4, core: 2. Of those that a mesh axis runs over, the one named last changes fastest.
Arguments:
- green: bfloat16 [4, 2, 8192, 8192], P('sweep', None, 'layer'), may hold values from -1 to 1
- down_source: float32 [4, 2, 16, 8192], P('sweep', None, None, 'layer'), may hold values from -6 to 6
- up_source: float32 [4, 2, 16, 8192], P('sweep', None, None, 'layer'), may hold values from -6 to 6
Outputs:
- total: float32 [4, 2, 16, 8192], P('sweep', None, None, 'layer')
All inputs are finite; a program needn't handle non-finite values.
Results may differ from a plain program's by a relative error of at most 0.02.
Values may be sent and summed in bfloat16 or wider, within the bound.
A program may use at most 64 MiB of HBM per device.

v0:
```python
import jax
import jax.numpy as jnp
from jax import lax
from jax.sharding import PartitionSpec as P


def from_behind(shard, axis, by):
    size = lax.axis_size(axis)
    pairs = [(i, i + by) for i in range(size) if 0 <= i + by < size]
    return lax.ppermute(shard, axis, pairs)


def rows_product(trace_in, matrix):
    contract = (((1,), (1,)), ((), ()))
    real_real = lax.dot_general(
        trace_in[0], matrix[0], contract, preferred_element_type=jnp.float32
    )
    imag_imag = lax.dot_general(
        trace_in[1], matrix[1], contract, preferred_element_type=jnp.float32
    )
    real_imag = lax.dot_general(
        trace_in[0], matrix[1], contract, preferred_element_type=jnp.float32
    )
    imag_real = lax.dot_general(
        trace_in[1], matrix[0], contract, preferred_element_type=jnp.float32
    )
    return jnp.stack([real_real - imag_imag, real_imag + imag_real])


def cols_product(trace_in, matrix):
    real_real = jnp.dot(trace_in[0], matrix[0], preferred_element_type=jnp.float32)
    imag_imag = jnp.dot(trace_in[1], matrix[1], preferred_element_type=jnp.float32)
    real_imag = jnp.dot(trace_in[0], matrix[1], preferred_element_type=jnp.float32)
    imag_real = jnp.dot(trace_in[1], matrix[0], preferred_element_type=jnp.float32)
    return jnp.stack([real_real - imag_imag, real_imag + imag_real])


def run_chain(own_term, product, passing, forward, blocks):
    count = lax.axis_size("sweep")
    my_index = lax.axis_index("sweep")
    position = my_index if forward else count - 1 - my_index
    width = own_term.shape[1] // blocks

    def turn(counter, state):
        result, incoming = state
        block_index = counter - position
        active = (block_index >= 0) & (block_index < blocks)
        update = own_term + product(incoming)
        previous = result
        result = jnp.where(active, update, previous)
        return (result, passing(update.astype(jnp.bfloat16)))

    start_state = (jnp.zeros_like(own_term), jnp.zeros((2, width, own_term.shape[2]), jnp.bfloat16))
    result, _unused = lax.fori_loop(0, count + blocks - 1, turn, start_state)
    return result


def local(green, down_source, up_source):
    matrix = green[0]
    blocks = 1

    def down_product(incoming):
        return rows_product(lax.all_gather(incoming, "layer", axis=2, tiled=True), matrix)

    def pass_down(outgoing):
        return from_behind(outgoing, "sweep", 1)

    downward = run_chain(down_source[0], down_product, pass_down, True, blocks)

    def up_product(incoming):
        return lax.psum_scatter(
            cols_product(incoming, matrix).astype(jnp.bfloat16),
            "layer",
            scatter_dimension=2,
            tiled=True,
        ).astype(jnp.float32)

    def pass_up(outgoing):
        return from_behind(outgoing, "sweep", -1)

    total = run_chain(up_source[0] + downward, up_product, pass_up, False, blocks)
    return total[None]


def solution(mesh):
    in_specs = (
        P("sweep", None, "layer", None),
        P("sweep", None, None, "layer"),
        P("sweep", None, None, "layer"),
    )
    out_specs = P("sweep", None, None, "layer")
    return jax.shard_map(local, mesh=mesh, in_specs=in_specs, out_specs=out_specs, check_vma=False)
```

profile of v0, /device:TPU:1, one launch (start us, length us, event | category | flops | bytes accessed | tf_op | source)
XLA Modules:
  0.0 484.3 jit_solution(7584108459187558484)
XLA Ops:
  6.5 192.2 %while.32 = (s32[]{:T(128)}, f32[2,16,1024]{2,1,0:T(8,128)S(1)}, bf16[2,16,1024]{2,1,0:T(8,128)(2,1)S(1)}, s32[]{:T(128)}, bf16[2,1024,8192]{2,1,0:T(8,128)(2,1)...) while((s32[]{:T(128)}, f32[2,16,1024]{2,1,0:T(8,128)S(1)}, ...), condition=%wide.region_1.2_spmd.clone, body=%wide.region_0.1_spmd.clone.sunk | while | flops 1073938432 | bytes 70516928 | solution.py:54
  6.6 11.3 %all_gather.9 = bf16[2,16,8192]{2,1,0:T(8,128)(2,1)S(1)} all-gather(bf16[2,16,1024]{2,1,0:T(8,128)(2,1)S(1)} %get-tuple-element.387), channel_id=1, replica_groups=mesh['sweep'=4,'layer'=8] {'layer'}, dimensions={2}, use_global_device_ids=true | all-gather | bytes 589824 | tf_op jit(solution)/shard_map/while/body/eval_jaxpr/all_gather | solution.py:63
  17.9 8.1 %fusion.92 = f32[16,1024]{1,0:T(8,128)S(1)} fusion(bf16[2,1024,8192]{2,1,0:T(8,128)(2,1)} %get-tuple-element.397, bf16[2,16,8192]{2,1,0:T(8,128)(2,1)S(1)} %all_gather.9), kind=kOutput, calls=%fused_computation.2.clone.1 | convolution fusion | flops 268435456 | bytes 17104896 | tf_op jit(solution)/shard_map/while/body/eval_jaxpr/dot_general | solution.py:18
  26.0 8.0 %fusion.90 = f32[16,1024]{1,0:T(8,128)S(1)} fusion(bf16[2,1024,8192]{2,1,0:T(8,128)(2,1)} %get-tuple-element.397, bf16[2,16,8192]{2,1,0:T(8,128)(2,1)S(1)} %all_gather.9), kind=kOutput, calls=%fused_computation.clone.1 | convolution fusion | flops 268435456 | bytes 17104896 | tf_op jit(solution)/shard_map/while/body/eval_jaxpr/dot_general | solution.py:21
  34.0 8.0 %fusion.93 = f32[1,16,1024]{2,1,0:T(8,128)S(1)} fusion(f32[16,1024]{1,0:T(8,128)S(1)} %fusion.92, bf16[2,1024,8192]{2,1,0:T(8,128)(2,1)} %get-tuple-element.397, bf16[2,16,8192]{2,1,0:T(8,128)(2,1)S(1)} %all_gather.9), kind=kOutput, calls=%fused_computation.13.clone.1 | convolution fusion | flops 268451840 | bytes 17170432 | tf_op jit(solution)/shard_map/while/body/eval_jaxpr/dot_general | solution.py:15
  42.0 8.0 %fusion.91 = f32[1,16,1024]{2,1,0:T(8,128)S(1)} fusion(f32[16,1024]{1,0:T(8,128)S(1)} %fusion.90, bf16[2,1024,8192]{2,1,0:T(8,128)(2,1)} %get-tuple-element.397, bf16[2,16,8192]{2,1,0:T(8,128)(2,1)S(1)} %all_gather.9), kind=kOutput, calls=%fused_computation.15.clone.1 | convolution fusion | flops 268451840 | bytes 17170432 | tf_op jit(solution)/shard_map/while/body/eval_jaxpr/dot_general | solution.py:24
  54.7 10.7 %all_gather.9 = bf16[2,16,8192]{2,1,0:T(8,128)(2,1)S(1)} all-gather(bf16[2,16,1024]{2,1,0:T(8,128)(2,1)S(1)} %get-tuple-element.387), channel_id=1, replica_groups=mesh['sweep'=4,'layer'=8] {'layer'}, dimensions={2}, use_global_device_ids=true | all-gather | bytes 589824 | tf_op jit(solution)/shard_map/while/body/eval_jaxpr/all_gather | solution.py:63
  65.4 8.1 %fusion.92 = f32[16,1024]{1,0:T(8,128)S(1)} fusion(bf16[2,1024,8192]{2,1,0:T(8,128)(2,1)} %get-tuple-element.397, bf16[2,16,8192]{2,1,0:T(8,128)(2,1)S(1)} %all_gather.9), kind=kOutput, calls=%fused_computation.2.clone.1 | convolution fusion | flops 268435456 | bytes 17104896 | tf_op jit(solution)/shard_map/while/body/eval_jaxpr/dot_general | solution.py:18
  73.4 8.0 %fusion.90 = f32[16,1024]{1,0:T(8,128)S(1)} fusion(bf16[2,1024,8192]{2,1,0:T(8,128)(2,1)} %get-tuple-element.397, bf16[2,16,8192]{2,1,0:T(8,128)(2,1)S(1)} %all_gather.9), kind=kOutput, calls=%fused_computation.clone.1 | convolution fusion | flops 268435456 | bytes 17104896 | tf_op jit(solution)/shard_map/while/body/eval_jaxpr/dot_general | solution.py:21
  81.5 8.0 %fusion.93 = f32[1,16,1024]{2,1,0:T(8,128)S(1)} fusion(f32[16,1024]{1,0:T(8,128)S(1)} %fusion.92, bf16[2,1024,8192]{2,1,0:T(8,128)(2,1)} %get-tuple-element.397, bf16[2,16,8192]{2,1,0:T(8,128)(2,1)S(1)} %all_gather.9), kind=kOutput, calls=%fused_computation.13.clone.1 | convolution fusion | flops 268451840 | bytes 17170432 | tf_op jit(solution)/shard_map/while/body/eval_jaxpr/dot_general | solution.py:15
  89.5 8.0 %fusion.91 = f32[1,16,1024]{2,1,0:T(8,128)S(1)} fusion(f32[16,1024]{1,0:T(8,128)S(1)} %fusion.90, bf16[2,1024,8192]{2,1,0:T(8,128)(2,1)} %get-tuple-element.397, bf16[2,16,8192]{2,1,0:T(8,128)(2,1)S(1)} %all_gather.9), kind=kOutput, calls=%fused_computation.15.clone.1 | convolution fusion | flops 268451840 | bytes 17170432 | tf_op jit(solution)/shard_map/while/body/eval_jaxpr/dot_general | solution.py:24
  103.0 9.7 %all_gather.9 = bf16[2,16,8192]{2,1,0:T(8,128)(2,1)S(1)} all-gather(bf16[2,16,1024]{2,1,0:T(8,128)(2,1)S(1)} %get-tuple-element.387), channel_id=1, replica_groups=mesh['sweep'=4,'layer'=8] {'layer'}, dimensions={2}, use_global_device_ids=true | all-gather | bytes 589824 | tf_op jit(solution)/shard_map/while/body/eval_jaxpr/all_gather | solution.py:63
  112.7 8.1 %fusion.92 = f32[16,1024]{1,0:T(8,128)S(1)} fusion(bf16[2,1024,8192]{2,1,0:T(8,128)(2,1)} %get-tuple-element.397, bf16[2,16,8192]{2,1,0:T(8,128)(2,1)S(1)} %all_gather.9), kind=kOutput, calls=%fused_computation.2.clone.1 | convolution fusion | flops 268435456 | bytes 17104896 | tf_op jit(solution)/shard_map/while/body/eval_jaxpr/dot_general | solution.py:18
  120.8 8.0 %fusion.90 = f32[16,1024]{1,0:T(8,128)S(1)} fusion(bf16[2,1024,8192]{2,1,0:T(8,128)(2,1)} %get-tuple-element.397, bf16[2,16,8192]{2,1,0:T(8,128)(2,1)S(1)} %all_gather.9), kind=kOutput, calls=%fused_computation.clone.1 | convolution fusion | flops 268435456 | bytes 17104896 | tf_op jit(solution)/shard_map/while/body/eval_jaxpr/dot_general | solution.py:21
  128.8 8.0 %fusion.93 = f32[1,16,1024]{2,1,0:T(8,128)S(1)} fusion(f32[16,1024]{1,0:T(8,128)S(1)} %fusion.92, bf16[2,1024,8192]{2,1,0:T(8,128)(2,1)} %get-tuple-element.397, bf16[2,16,8192]{2,1,0:T(8,128)(2,1)S(1)} %all_gather.9), kind=kOutput, calls=%fused_computation.13.clone.1 | convolution fusion | flops 268451840 | bytes 17170432 | tf_op jit(solution)/shard_map/while/body/eval_jaxpr/dot_general | solution.py:15
  136.9 8.0 %fusion.91 = f32[1,16,1024]{2,1,0:T(8,128)S(1)} fusion(f32[16,1024]{1,0:T(8,128)S(1)} %fusion.90, bf16[2,1024,8192]{2,1,0:T(8,128)(2,1)} %get-tuple-element.397, bf16[2,16,8192]{2,1,0:T(8,128)(2,1)S(1)} %all_gather.9), kind=kOutput, calls=%fused_computation.15.clone.1 | convolution fusion | flops 268451840 | bytes 17170432 | tf_op jit(solution)/shard_map/while/body/eval_jaxpr/dot_general | solution.py:24
  150.4 10.7 %all_gather.9 = bf16[2,16,8192]{2,1,0:T(8,128)(2,1)S(1)} all-gather(bf16[2,16,1024]{2,1,0:T(8,128)(2,1)S(1)} %get-tuple-element.387), channel_id=1, replica_groups=mesh['sweep'=4,'layer'=8] {'layer'}, dimensions={2}, use_global_device_ids=true | all-gather | bytes 589824 | tf_op jit(solution)/shard_map/while/body/eval_jaxpr/all_gather | solution.py:63
  161.1 8.1 %fusion.92 = f32[16,1024]{1,0:T(8,128)S(1)} fusion(bf16[2,1024,8192]{2,1,0:T(8,128)(2,1)} %get-tuple-element.397, bf16[2,16,8192]{2,1,0:T(8,128)(2,1)S(1)} %all_gather.9), kind=kOutput, calls=%fused_computation.2.clone.1 | convolution fusion | flops 268435456 | bytes 17104896 | tf_op jit(solution)/shard_map/while/body/eval_jaxpr/dot_general | solution.py:18
  169.1 8.0 %fusion.90 = f32[16,1024]{1,0:T(8,128)S(1)} fusion(bf16[2,1024,8192]{2,1,0:T(8,128)(2,1)} %get-tuple-element.397, bf16[2,16,8192]{2,1,0:T(8,128)(2,1)S(1)} %all_gather.9), kind=kOutput, calls=%fused_computation.clone.1 | convolution fusion | flops 268435456 | bytes 17104896 | tf_op jit(solution)/shard_map/while/body/eval_jaxpr/dot_general | solution.py:21
  177.2 8.0 %fusion.93 = f32[1,16,1024]{2,1,0:T(8,128)S(1)} fusion(f32[16,1024]{1,0:T(8,128)S(1)} %fusion.92, bf16[2,1024,8192]{2,1,0:T(8,128)(2,1)} %get-tuple-element.397, bf16[2,16,8192]{2,1,0:T(8,128)(2,1)S(1)} %all_gather.9), kind=kOutput, calls=%fused_computation.13.clone.1 | convolution fusion | flops 268451840 | bytes 17170432 | tf_op jit(solution)/shard_map/while/body/eval_jaxpr/dot_general | solution.py:15
  185.2 8.0 %fusion.91 = f32[1,16,1024]{2,1,0:T(8,128)S(1)} fusion(f32[16,1024]{1,0:T(8,128)S(1)} %fusion.90, bf16[2,1024,8192]{2,1,0:T(8,128)(2,1)} %get-tuple-element.397, bf16[2,16,8192]{2,1,0:T(8,128)(2,1)S(1)} %all_gather.9), kind=kOutput, calls=%fused_computation.15.clone.1 | convolution fusion | flops 268451840 | bytes 17170432 | tf_op jit(solution)/shard_map/while/body/eval_jaxpr/dot_general | solution.py:24
  198.8 278.3 %while.33 = (s32[]{:T(128)}, f32[2,16,1024]{2,1,0:T(8,128)S(1)}, bf16[2,16,1024]{2,1,0:T(8,128)(2,1)S(1)}, s32[]{:T(128)}, bf16[2,1024,8192]{2,1,0:T(8,128)(2,1)...) while((s32[]{:T(128)}, f32[2,16,1024]{2,1,0:T(8,128)S(1)}, ...), condition=%wide.region_4.5_spmd.clone, body=%wide.region_2.4_spmd.clone.sunk | while | flops 1074692096 | bytes 73466064 | solution.py:54
  220.0 7.0 %fusion.106 = bf16[1,16,8192]{2,1,0:T(8,128)(2,1)S(1)} fusion(f32[16,8192]{1,0:T(8,128)S(1)} %fusion.105, bf16[2,1024,8192]{2,1,0:T(8,128)(2,1)} %get-tuple-element.421, bf16[2,16,1024]{2,1,0:T(8,128)(2,1)S(1)} %get-tuple-element.411), kind=kOutput, calls=%fused_computation.37.clone.1 | convolution fusion | flops 268697600 | bytes 17596416 | tf_op jit(solution)/shard_map/while/body/eval_jaxpr/dot_general | solution.py:31
  228.0 35.2 %reduce-scatter.2.cloned.1.call-done = bf16[2,16,1024]{2,1,0:T(8,128)(2,1)} async-done(((bf16[2,16,8192]{2,1,0:T(8,128)(2,1)}), bf16[2,16,1024]{2,1,0:T(8,128)(2,1)}) %reduce-scatter.2.cloned.1.call-update) | async-done | bytes 65552 | tf_op jit(solution)/shard_map/while/body/eval_jaxpr/reduce_scatter | solution.py:71
  283.0 7.0 %fusion.104 = bf16[1,16,8192]{2,1,0:T(8,128)(2,1)S(1)} fusion(f32[16,8192]{1,0:T(8,128)S(1)} %fusion.103, bf16[2,1024,8192]{2,1,0:T(8,128)(2,1)} %get-tuple-element.421, bf16[2,16,1024]{2,1,0:T(8,128)(2,1)S(1)} %get-tuple-element.411), kind=kOutput, calls=%fused_computation.38.clone.1 | convolution fusion | flops 268697600 | bytes 17596416 | tf_op jit(solution)/shard_map/while/body/eval_jaxpr/dot_general | solution.py:34
  290.1 7.0 %fusion.106 = bf16[1,16,8192]{2,1,0:T(8,128)(2,1)S(1)} fusion(f32[16,8192]{1,0:T(8,128)S(1)} %fusion.105, bf16[2,1024,8192]{2,1,0:T(8,128)(2,1)} %get-tuple-element.421, bf16[2,16,1024]{2,1,0:T(8,128)(2,1)S(1)} %get-tuple-element.411), kind=kOutput, calls=%fused_computation.37.clone.1 | convolution fusion | flops 268697600 | bytes 17596416 | tf_op jit(solution)/shard_map/while/body/eval_jaxpr/dot_general | solution.py:31
  298.0 34.5 %reduce-scatter.2.cloned.1.call-done = bf16[2,16,1024]{2,1,0:T(8,128)(2,1)} async-done(((bf16[2,16,8192]{2,1,0:T(8,128)(2,1)}), bf16[2,16,1024]{2,1,0:T(8,128)(2,1)}) %reduce-scatter.2.cloned.1.call-update) | async-done | bytes 65552 | tf_op jit(solution)/shard_map/while/body/eval_jaxpr/reduce_scatter | solution.py:71
  352.3 7.0 %fusion.104 = bf16[1,16,8192]{2,1,0:T(8,128)(2,1)S(1)} fusion(f32[16,8192]{1,0:T(8,128)S(1)} %fusion.103, bf16[2,1024,8192]{2,1,0:T(8,128)(2,1)} %get-tuple-element.421, bf16[2,16,1024]{2,1,0:T(8,128)(2,1)S(1)} %get-tuple-element.411), kind=kOutput, calls=%fused_computation.38.clone.1 | convolution fusion | flops 268697600 | bytes 17596416 | tf_op jit(solution)/shard_map/while/body/eval_jaxpr/dot_general | solution.py:34
  359.4 7.0 %fusion.106 = bf16[1,16,8192]{2,1,0:T(8,128)(2,1)S(1)} fusion(f32[16,8192]{1,0:T(8,128)S(1)} %fusion.105, bf16[2,1024,8192]{2,1,0:T(8,128)(2,1)} %get-tuple-element.421, bf16[2,16,1024]{2,1,0:T(8,128)(2,1)S(1)} %get-tuple-element.411), kind=kOutput, calls=%fused_computation.37.clone.1 | convolution fusion | flops 268697600 | bytes 17596416 | tf_op jit(solution)/shard_map/while/body/eval_jaxpr/dot_general | solution.py:31
  367.3 34.5 %reduce-scatter.2.cloned.1.call-done = bf16[2,16,1024]{2,1,0:T(8,128)(2,1)} async-done(((bf16[2,16,8192]{2,1,0:T(8,128)(2,1)}), bf16[2,16,1024]{2,1,0:T(8,128)(2,1)}) %reduce-scatter.2.cloned.1.call-update) | async-done | bytes 65552 | tf_op jit(solution)/shard_map/while/body/eval_jaxpr/reduce_scatter | solution.py:71
  428.7 7.0 %fusion.106 = bf16[1,16,8192]{2,1,0:T(8,128)(2,1)S(1)} fusion(f32[16,8192]{1,0:T(8,128)S(1)} %fusion.105, bf16[2,1024,8192]{2,1,0:T(8,128)(2,1)} %get-tuple-element.421, bf16[2,16,1024]{2,1,0:T(8,128)(2,1)S(1)} %get-tuple-element.411), kind=kOutput, calls=%fused_computation.37.clone.1 | convolution fusion | flops 268697600 | bytes 17596416 | tf_op jit(solution)/shard_map/while/body/eval_jaxpr/dot_general | solution.py:31
  436.7 34.5 %reduce-scatter.2.cloned.1.call-done = bf16[2,16,1024]{2,1,0:T(8,128)(2,1)} async-done(((bf16[2,16,8192]{2,1,0:T(8,128)(2,1)}), bf16[2,16,1024]{2,1,0:T(8,128)(2,1)}) %reduce-scatter.2.cloned.1.call-update) | async-done | bytes 65552 | tf_op jit(solution)/shard_map/while/body/eval_jaxpr/reduce_scatter | solution.py:71
  (63 shorter events, 118.5 us)
Async XLA Ops:
  6.5 192.2 %copy-start.2 = (f32[1,2,16,1024]{3,2,1,0:T(8,128)S(1)}, f32[1,2,16,1024]{3,2,1,0:T(8,128)}, u32[]{:S(2)}) copy-start(f32[1,2,16,1024]{3,2,1,0:T(8,128)} %param.9) | copy-start | bytes 393220
  17.9 32.2 %copy-start = (f32[2,16,1024]{2,1,0:T(8,128)S(1)}, f32[2,16,1024]{2,1,0:T(8,128)}, u32[]{:S(2)}) copy-start(f32[2,16,1024]{2,1,0:T(8,128)} %get-tuple-element.398) | copy-start | bytes 393220 | tf_op jit(solution)/shard_map/while
  50.2 4.5 collective-permute-start
  65.4 32.2 %copy-start = (f32[2,16,1024]{2,1,0:T(8,128)S(1)}, f32[2,16,1024]{2,1,0:T(8,128)}, u32[]{:S(2)}) copy-start(f32[2,16,1024]{2,1,0:T(8,128)} %get-tuple-element.398) | copy-start | bytes 393220 | tf_op jit(solution)/shard_map/while
  97.6 5.4 %collective-permute-start = (bf16[2,16,1024]{2,1,0:T(8,128)(2,1)S(1)}, bf16[2,16,1024]{2,1,0:T(8,128)(2,1)S(1)}, u32[]{:S(2)}, u32[]{:S(2)}) collective-permute-start(bf16[2,16,1024]{2,1,0:T(8,128)(2,1)S(1)} %get-tuple-element.368), channel_id=1, source_target_pairs={{0,8},{8,16},{16,24},{1,9},{9,17},{17,25},{2,10},{10,18},{18,26},{... | collective-permute-start | bytes 196616 | tf_op jit(solution)/shard_map/while/body/eval_jaxpr/ppermute | solution.py:10
  112.7 32.2 %copy-start = (f32[2,16,1024]{2,1,0:T(8,128)S(1)}, f32[2,16,1024]{2,1,0:T(8,128)}, u32[]{:S(2)}) copy-start(f32[2,16,1024]{2,1,0:T(8,128)} %get-tuple-element.398) | copy-start | bytes 393220 | tf_op jit(solution)/shard_map/while
  145.0 5.4 %collective-permute-start = (bf16[2,16,1024]{2,1,0:T(8,128)(2,1)S(1)}, bf16[2,16,1024]{2,1,0:T(8,128)(2,1)S(1)}, u32[]{:S(2)}, u32[]{:S(2)}) collective-permute-start(bf16[2,16,1024]{2,1,0:T(8,128)(2,1)S(1)} %get-tuple-element.368), channel_id=1, source_target_pairs={{0,8},{8,16},{16,24},{1,9},{9,17},{17,25},{2,10},{10,18},{18,26},{... | collective-permute-start | bytes 196616 | tf_op jit(solution)/shard_map/while/body/eval_jaxpr/ppermute | solution.py:10
  161.1 32.2 %copy-start = (f32[2,16,1024]{2,1,0:T(8,128)S(1)}, f32[2,16,1024]{2,1,0:T(8,128)}, u32[]{:S(2)}) copy-start(f32[2,16,1024]{2,1,0:T(8,128)} %get-tuple-element.398) | copy-start | bytes 393220 | tf_op jit(solution)/shard_map/while
  193.3 5.4 %collective-permute-start = (bf16[2,16,1024]{2,1,0:T(8,128)(2,1)S(1)}, bf16[2,16,1024]{2,1,0:T(8,128)(2,1)S(1)}, u32[]{:S(2)}, u32[]{:S(2)}) collective-permute-start(bf16[2,16,1024]{2,1,0:T(8,128)(2,1)S(1)} %get-tuple-element.368), channel_id=1, source_target_pairs={{0,8},{8,16},{16,24},{1,9},{9,17},{17,25},{2,10},{10,18},{18,26},{... | collective-permute-start | bytes 196616 | tf_op jit(solution)/shard_map/while/body/eval_jaxpr/ppermute | solution.py:10
  199.0 64.2 %reduce-scatter.2.cloned.1.call-start = ((), (), s32[]{:S(2)}) async-start(), calls=%async_computation.1 | async-start | bytes 589824 | tf_op jit(solution)/shard_map/while/body/eval_jaxpr/reduce_scatter | solution.py:71
  264.1 5.0 %collective-permute-start.1 = (bf16[2,16,1024]{2,1,0:T(8,128)(2,1)S(1)}, bf16[2,16,1024]{2,1,0:T(8,128)(2,1)S(1)}, u32[]{:S(2)}, u32[]{:S(2)}) collective-permute-start(bf16[2,16,1024]{2,1,0:T(8,128)(2,1)S(1)} %get-tuple-element.376), channel_id=1, source_target_pairs={{8,0},{16,8},{24,16},{9,1},{17,9},{25,17},{10,2},{18,10},{26,18},{... | collective-permute-start | bytes 196616 | tf_op jit(solution)/shard_map/while/body/eval_jaxpr/ppermute | solution.py:10
  269.1 63.4 %reduce-scatter.2.cloned.1.call-start = ((), (), s32[]{:S(2)}) async-start(), calls=%async_computation.1 | async-start | bytes 589824 | tf_op jit(solution)/shard_map/while/body/eval_jaxpr/reduce_scatter | solution.py:71
  333.4 5.0 %collective-permute-start.1 = (bf16[2,16,1024]{2,1,0:T(8,128)(2,1)S(1)}, bf16[2,16,1024]{2,1,0:T(8,128)(2,1)S(1)}, u32[]{:S(2)}, u32[]{:S(2)}) collective-permute-start(bf16[2,16,1024]{2,1,0:T(8,128)(2,1)S(1)} %get-tuple-element.376), channel_id=1, source_target_pairs={{8,0},{16,8},{24,16},{9,1},{17,9},{25,17},{10,2},{18,10},{26,18},{... | collective-permute-start | bytes 196616 | tf_op jit(solution)/shard_map/while/body/eval_jaxpr/ppermute | solution.py:10
  338.4 63.4 %reduce-scatter.2.cloned.1.call-start = ((), (), s32[]{:S(2)}) async-start(), calls=%async_computation.1 | async-start | bytes 589824 | tf_op jit(solution)/shard_map/while/body/eval_jaxpr/reduce_scatter | solution.py:71
  402.7 5.0 %collective-permute-start.1 = (bf16[2,16,1024]{2,1,0:T(8,128)(2,1)S(1)}, bf16[2,16,1024]{2,1,0:T(8,128)(2,1)S(1)}, u32[]{:S(2)}, u32[]{:S(2)}) collective-permute-start(bf16[2,16,1024]{2,1,0:T(8,128)(2,1)S(1)} %get-tuple-element.376), channel_id=1, source_target_pairs={{8,0},{16,8},{24,16},{9,1},{17,9},{25,17},{10,2},{18,10},{26,18},{... | collective-permute-start | bytes 196616 | tf_op jit(solution)/shard_map/while/body/eval_jaxpr/ppermute | solution.py:10
  407.7 63.4 %reduce-scatter.2.cloned.1.call-start = ((), (), s32[]{:S(2)}) async-start(), calls=%async_computation.1 | async-start | bytes 589824 | tf_op jit(solution)/shard_map/while/body/eval_jaxpr/reduce_scatter | solution.py:71
  472.1 5.0 %collective-permute-start.1 = (bf16[2,16,1024]{2,1,0:T(8,128)(2,1)S(1)}, bf16[2,16,1024]{2,1,0:T(8,128)(2,1)S(1)}, u32[]{:S(2)}, u32[]{:S(2)}) collective-permute-start(bf16[2,16,1024]{2,1,0:T(8,128)(2,1)S(1)} %get-tuple-element.376), channel_id=1, source_target_pairs={{8,0},{16,8},{24,16},{9,1},{17,9},{25,17},{10,2},{18,10},{26,18},{... | collective-permute-start | bytes 196616 | tf_op jit(solution)/shard_map/while/body/eval_jaxpr/ppermute | solution.py:10
  477.1 0.7 copy-start.1
Sparse Core Ops, SparseCore 0:
  228.1 35.0 reduce-scatter.1
  298.1 34.3 reduce-scatter.1
  367.4 34.3 reduce-scatter.1
  436.8 34.3 reduce-scatter.1
where the time goes:
time: 487 us; the launch traced here: 484 us
  matrix products  241 us (49%)
  waiting for transfers between devices  159 us (33%)
  blocking collectives  42.4 us (9%)
  starting transfers between devices  20.6 us (4%)
  between operations  13.1 us (3%)
  other arithmetic  7.22 us (1%)
    reduce_scatter x4, waiting for transfers between devices, up_product(): lax.psum_scatter(cols_product(incoming, matrix).astype(jnp.bfloat16), 'la...  139 us
    all_gather x4, blocking collectives, down_product(): lax.all_gather(incoming, 'layer', axis=2, tiled=True)  42.4 us
    dot_general x4, matrix products, rows_product(): lax.dot_general(trace_in[1], matrix[1], contract, preferred_element_type=...  32.3 us
    dot_general x4, matrix products, rows_product(): lax.dot_general(trace_in[1], matrix[0], contract, preferred_element_type=...  32.2 us
    dot_general x4, matrix products, rows_product(): lax.dot_general(trace_in[0], matrix[0], contract, preferred_element_type=...  32.2 us
    dot_general x4, matrix products, rows_product(): lax.dot_general(trace_in[0], matrix[1], contract, preferred_element_type=...  32.2 us
    dot_general x4, matrix products, cols_product(): jnp.dot(trace_in[0], matrix[0], preferred_element_type=jnp.float32)  28.2 us
    dot_general x4, matrix products, cols_product(): jnp.dot(trace_in[1], matrix[0], preferred_element_type=jnp.float32)  28.2 us
  transfers between devices with their start and end apart: 12, of which 12 were waited for; matrix products, arithmetic and copies ran while one was open for 0% of the time, Pallas kernels for 0%

commit v1 on v0

v1 whole, which is shorter than its diff:
```python
import functools

import jax
import jax.numpy as jnp
from jax import lax
from jax.experimental import pallas as pl
from jax.experimental.pallas import tpu as pltpu
from jax.sharding import PartitionSpec as P

MESH = pl.DeviceIdType.MESH
F32, BF16 = jnp.float32, jnp.bfloat16
BY_LANES = (((1,), (1,)), ((), ()))


def turned(trace):
    half = trace.shape[0] // 2
    return jnp.concatenate([-trace[half:], trace[:half]], axis=0)


def rows_dot(trace, block):
    return lax.dot_general(trace, block, BY_LANES, preferred_element_type=F32)


def cols_dot(trace, block):
    return jnp.dot(trace, block, preferred_element_type=F32)


def sweeps(layers, peers, blocks, green, down_src, up_src, total,
           matrix, gathered, incoming, part_out, part_in, out_down, out_up, base, acc,
           load_sem, dsend, drecv, gsend, grecv, usend, urecv, psend, precv):
    z, j = lax.axis_index("sweep"), lax.axis_index("layer")
    own = down_src.shape[1]
    width = own // blocks
    odd = lax.rem(z, 2) == 1

    def span(k):
        return pl.ds(pl.multiple_of(k * width, width), width)

    def cols(i, k):
        return pl.ds(pl.multiple_of(i * own + k * width, width), width)

    def peer(d):
        return lax.rem(j + d, peers)

    def load(m, part):
        return pltpu.make_async_copy(
            green.at[part, span(m)], matrix.at[part, span(m)], load_sem.at[m, part])

    def wait_load(m):
        load(m, 0).wait()
        load(m, 1).wait()

    def remote(src, dst, send, recv, to):
        return pltpu.make_async_remote_copy(
            src_ref=src, dst_ref=dst, send_sem=send, recv_sem=recv, device_id=to, device_id_type=MESH)

    def pass_down(k):
        return remote(out_down.at[k], gathered.at[k, j], dsend.at[k], drecv.at[k], {"sweep": z + 1})

    def pass_up(k):
        return remote(out_up.at[k], incoming.at[k], usend.at[k], urecv.at[k], {"sweep": z - 1})

    def relay(k, d):
        return remote(gathered.at[k, j], gathered.at[k, j], gsend.at[k, d], grecv.at[k, j], {"layer": peer(d)})

    def relayed(k, d):
        i = peer(d)
        return remote(gathered.at[k, i], gathered.at[k, i], gsend.at[k, d], grecv.at[k, i], {"layer": i})

    def share(d, k):
        i = peer(d)
        return remote(part_out.at[i, k], part_in.at[j, k], psend.at[d, k], precv.at[j, k], {"layer": i})

    def shared(d, k):
        i = peer(d)
        return remote(part_out.at[i, k], part_in.at[i, k], psend.at[d, k], precv.at[i, k], {"layer": i})

    def share_all(d):
        i = peer(d)
        return remote(part_out.at[i], part_in.at[j], psend.at[d, 0], precv.at[j, 0], {"layer": i})

    def shared_all(d):
        i = peer(d)
        return remote(part_out.at[i], part_in.at[i], psend.at[d, 0], precv.at[i, 0], {"layer": i})

    for m in range(blocks):
        load(m, 0).start()
        load(m, 1).start()

    barrier = pltpu.get_barrier_semaphore()
    for d in range(1, peers):
        pl.semaphore_signal(barrier, inc=1, device_id={"layer": peer(d)}, device_id_type=MESH)
    for step in (1, layers - 1):
        pl.semaphore_signal(barrier, inc=1, device_id={"sweep": lax.rem(z + step, layers)}, device_id_type=MESH)
    pl.semaphore_wait(barrier, peers + 1)

    def finish_down(k, value):
        sum_of = up_src[:, span(k)] + value

        @pl.when(z < layers - 1)
        def _():
            base[:, span(k)] = sum_of
            out_down[k] = value.astype(BF16)
            pass_down(k).start()

        @pl.when(z == layers - 1)
        def _():
            total[:, span(k)] = sum_of
            out_up[k] = sum_of.astype(BF16)
            pass_up(k).start()

    def take(k):
        relayed_own = remote(
            out_down.at[k], gathered.at[k, j], dsend.at[k], drecv.at[k], {"sweep": z})
        relayed_own.wait_recv()
        for d in range(1, peers):
            relay(k, d).start()

    def wait_gather(k):
        for d in range(1, peers):
            relayed(k, d).wait_recv()

    def wait_up(k):
        remote(out_up.at[k], incoming.at[k], usend.at[k], urecv.at[k], {"sweep": z}).wait_recv()

    @pl.when(z == 0)
    def _():
        @pl.loop(0, blocks)
        def _(k):
            finish_down(k, down_src[:, span(k)])

        @pl.loop(0, blocks)
        def _(m):
            wait_load(m)

    @pl.when(odd)
    def _():
        @pl.loop(0, blocks)
        def _(k):
            take(k)

        @pl.loop(0, blocks)
        def _(k):
            wait_gather(k)

        @pl.loop(0, blocks)
        def _(m):
            wait_load(m)
            value = None
            for k in range(blocks):
                for i in range(peers):
                    trace = gathered[k, i]
                    term = rows_dot(trace, matrix[0, span(m), cols(i, k)])
                    value = term if value is None else value + term
                    value = value + rows_dot(turned(trace), matrix[1, span(m), cols(i, k)])
            finish_down(m, down_src[:, span(m)] + value)

    @pl.when(jnp.logical_not(odd) & (z > 0))
    def _():
        @pl.loop(0, blocks)
        def _(m):
            wait_load(m)

        base[...] = down_src[...]
        take(0)

        @pl.loop(0, blocks)
        def _(k):
            @pl.when(k + 1 < blocks)
            def _():
                take(k + 1)

            wait_gather(k)
            for m in range(blocks):
                value = None
                for i in range(peers):
                    trace = gathered[k, i]
                    term = rows_dot(trace, matrix[0, span(m), cols(i, k)])
                    value = term if value is None else value + term
                    value = value + rows_dot(turned(trace), matrix[1, span(m), cols(i, k)])
                base[:, span(m)] += value

        @pl.loop(0, blocks)
        def _(k):
            finish_down(k, base[:, span(k)])

    def finish_up(k):
        value = acc[j, :, span(k)]
        for d in range(1, peers):
            value = value + part_in[peer(d), k].astype(F32)
        value = base[:, span(k)] + value
        total[:, span(k)] = value

        @pl.when(z > 0)
        def _():
            out_up[k] = value.astype(BF16)
            pass_up(k).start()

    @pl.when(odd & (z < layers - 1))
    def _():
        @pl.loop(0, blocks)
        def _(k):
            wait_up(k)

        def reduce(k):
            for d in range(1, peers):
                shared(d, k).wait_recv()
            finish_up(k)

        @pl.loop(0, blocks)
        def _(k):
            for d in list(range(1, peers)) + [0]:
                i = peer(d)
                value = None
                for r in range(blocks):
                    trace = incoming[r]
                    term = cols_dot(trace, matrix[0, span(r), cols(i, k)])
                    value = term if value is None else value + term
                    value = value + cols_dot(turned(trace), matrix[1, span(r), cols(i, k)])
                if d:
                    part_out[i, k] = value.astype(BF16)
                else:
                    acc[i, :, span(k)] = value
            for d in range(1, peers):
                share(d, k).start()

            @pl.when(k > 0)
            def _():
                reduce(k - 1)

        reduce(blocks - 1)

        @pl.loop(0, blocks)
        def _(k):
            for d in range(1, peers):
                share(d, k).wait_send()

    @pl.when(jnp.logical_not(odd) & (z < layers - 1))
    def _():
        acc[...] = jnp.zeros_like(acc)

        @pl.loop(0, blocks)
        def _(r):
            wait_up(r)
            trace = incoming[r]
            for i in range(peers):
                for k in range(blocks):
                    value = cols_dot(trace, matrix[0, span(r), cols(i, k)])
                    value = value + cols_dot(turned(trace), matrix[1, span(r), cols(i, k)])
                    acc[i, :, span(k)] += value

        for d in range(1, peers):
            i = peer(d)
            for k in range(blocks):
                part_out[i, k] = acc[i, :, span(k)].astype(BF16)
            share_all(d).start()
        for d in range(1, peers):
            shared_all(d).wait_recv()

        @pl.loop(0, blocks)
        def _(k):
            finish_up(k)

        for d in range(1, peers):
            share_all(d).wait_send()

    @pl.when(z < layers - 1)
    def _():
        @pl.loop(0, blocks)
        def _(k):
            pass_down(k).wait_send()

    @pl.when(z > 0)
    def _():
        @pl.loop(0, blocks)
        def _(k):
            pass_up(k).wait_send()
            for d in range(1, peers):
                relay(k, d).wait_send()


def local(layers, peers, green, down_source, up_source):
    _one, parts, own, wide = green.shape
    sources = down_source.shape[2]
    both = parts * sources
    blocks = next(b for b in (4, 2, 1) if own % (b * 128) == 0)
    width = own // blocks
    vmem = pl.BlockSpec(memory_space=pltpu.VMEM)
    dma = pltpu.SemaphoreType.DMA
    result = pl.pallas_call(
        functools.partial(sweeps, layers, peers, blocks),
        out_shape=jax.ShapeDtypeStruct((both, own), F32),
        in_specs=[pl.BlockSpec(memory_space=pl.ANY), vmem, vmem],
        out_specs=vmem,
        scratch_shapes=[
            pltpu.VMEM((parts, own, wide), BF16),
            pltpu.VMEM((blocks, peers, both, width), BF16),
            pltpu.VMEM((blocks, both, width), BF16),
            pltpu.VMEM((peers, blocks, both, width), BF16),
            pltpu.VMEM((peers, blocks, both, width), BF16),
            pltpu.VMEM((blocks, both, width), BF16),
            pltpu.VMEM((blocks, both, width), BF16),
            pltpu.VMEM((both, own), F32),
            pltpu.VMEM((peers, both, own), F32),
            dma((blocks, 2)),
            dma((blocks,)), dma((blocks,)),
            dma((blocks, peers)), dma((blocks, peers)),
            dma((blocks,)), dma((blocks,)),
            dma((peers, blocks)), dma((peers, blocks)),
        ],
        compiler_params=pltpu.CompilerParams(
            collective_id=0, has_side_effects=True, vmem_limit_bytes=60 * 1024 * 1024),
    )(green[0], down_source.reshape(both, own), up_source.reshape(both, own))
    return result.reshape(1, parts, sources, own)


def solution(mesh):
    in_specs = (
        P("sweep", None, "layer", None),
        P("sweep", None, None, "layer"),
        P("sweep", None, None, "layer"),
    )
    out_specs = P("sweep", None, None, "layer")
    body = functools.partial(local, mesh.shape["sweep"], mesh.shape["layer"])
    return jax.shard_map(body, mesh=mesh, in_specs=in_specs, out_specs=out_specs, check_vma=False)
```

time: 487 us -> 95.5 us (0.20)
  matrix products: 241 us -> 0 us
  waiting for transfers between devices: 159 us -> 0 us
  Pallas kernels: 0 us -> 93.8 us
  blocking collectives: 42.4 us -> 0 us
  starting transfers between devices: 20.6 us -> 0 us
  between operations: 13.1 us -> 0.01 us
  other arithmetic: 7.22 us -> 0 us
    dot_general x32 -> x0, matrix products: 241 us -> none  [the longest x4 32.3 us: rows_product(): lax.dot_general(trace_in[1], matrix[1], contract, preferred_element_type=...]
    reduce_scatter x4 -> x0, waiting for transfers between devices: 139 us -> none  [up_product(): lax.psum_scatter(cols_product(incoming, matrix).astype(jnp.bfloat16), 'la...]
    pallas_call x0 -> x1, Pallas kernels: none -> 93.8 us  [local(): pl.pallas_call(functools.partial(sweeps, layers, peers, blocks), out_shap...]
    all_gather x4 -> x0, blocking collectives: 42.4 us -> none  [down_product(): lax.all_gather(incoming, 'layer', axis=2, tiled=True)]
    ppermute x8 -> x0, starting transfers between devices: 20.6 us -> none  [from_behind(): return lax.ppermute(shard, axis, pairs)]
    ppermute x8 -> x0, waiting for transfers between devices: 20.1 us -> none  [from_behind(): return lax.ppermute(shard, axis, pairs)]
  transfers between devices with their start and end apart: 12 -> 0, of which waited for: 12 -> 0; matrix products, arithmetic and copies ran while one was open for 0% -> 0% of each run, Pallas kernels for 0% -> 0%
where the time goes in v1:
time: 95.5 us; the launch traced here: 95.4 us
  Pallas kernels  93.8 us (98%)
  local copies, waits for them, and re-layouts  1.57 us (2%)
    pallas_call x1, Pallas kernels, local(): pl.pallas_call(functools.partial(sweeps, layers, peers, blocks), out_shap...  93.8 us

profile of v1, /device:TPU:1, one launch (start us, length us, event | category | flops | bytes accessed | tf_op | source)
XLA Modules:
  0.0 95.4 jit_solution(11239738905098901292)
XLA Ops:
  0.0 93.8 %shard_map.37 = f32[32,1024]{1,0:T(8,128)} custom-call(bf16[2,1024,8192]{2,1,0:T(8,128)(2,1)} %bitcast.4, f32[32,1024]{1,0:T(8,128)} %bitcast.6, f32[32,1024]{1,0:T(8,128)} %bitcast.7), custom_call_target="tpu_custom_call" | custom-call | tf_op jit(solution)/shard_map/pallas_call | solution.py:290
  93.8 1.6 %copy.5 = f32[1,2,16,1024]{3,2,1,0:T(8,128)} copy(f32[1,2,16,1024]{3,2,1,0:T(8,128)} %bitcast.5) | data formatting | bytes 262144

commit v2 on v1

--- a/solution.py
+++ b/solution.py
@@ -123,6 +123,16 @@
     def wait_up(k):
         remote(out_up.at[k], incoming.at[k], usend.at[k], urecv.at[k], {"sweep": z}).wait_recv()
 
+    def down_term(m, ks):
+        value = None
+        for k in ks:
+            for i in range(peers):
+                trace = gathered[k, i]
+                term = rows_dot(trace, matrix[0, span(m), cols(i, k)])
+                value = term if value is None else value + term
+                value = value + rows_dot(turned(trace), matrix[1, span(m), cols(i, k)])
+        return value
+
     @pl.when(z == 0)
     def _():
         @pl.loop(0, blocks)
@@ -133,7 +143,7 @@
         def _(m):
             wait_load(m)
 
-    @pl.when(odd)
+    @pl.when(z == 1)
     def _():
         @pl.loop(0, blocks)
         def _(k):
@@ -146,14 +156,35 @@
         @pl.loop(0, blocks)
         def _(m):
             wait_load(m)
-            value = None
-            for k in range(blocks):
-                for i in range(peers):
-                    trace = gathered[k, i]
-                    term = rows_dot(trace, matrix[0, span(m), cols(i, k)])
-                    value = term if value is None else value + term
-                    value = value + rows_dot(turned(trace), matrix[1, span(m), cols(i, k)])
-            finish_down(m, down_src[:, span(m)] + value)
+            finish_down(m, down_src[:, span(m)] + down_term(m, range(blocks)))
+
+    @pl.when(odd & (z > 1))
+    def _():
+        early = blocks // 2
+
+        @pl.loop(0, blocks)
+        def _(m):
+            wait_load(m)
+
+        base[...] = down_src[...]
+
+        @pl.loop(0, blocks)
+        def _(k):
+            take(k)
+
+        @pl.loop(0, early)
+        def _(k):
+            wait_gather(k)
+            for m in range(blocks):
+                base[:, span(m)] += down_term(m, [k])
+
+        @pl.loop(early, blocks)
+        def _(k):
+            wait_gather(k)
+
+        @pl.loop(0, blocks)
+        def _(m):
+            finish_down(m, base[:, span(m)] + down_term(m, range(early, blocks)))
 
     @pl.when(jnp.logical_not(odd) & (z > 0))
     def _():
@@ -164,25 +195,16 @@
         base[...] = down_src[...]
         take(0)
 
-        @pl.loop(0, blocks)
-        def _(k):
-            @pl.when(k + 1 < blocks)
-            def _():
-                take(k + 1)
-
+        @pl.loop(0, blocks - 1)
+        def _(k):
+            take(k + 1)
             wait_gather(k)
             for m in range(blocks):
-                value = None
-                for i in range(peers):
-                    trace = gathered[k, i]
-                    term = rows_dot(trace, matrix[0, span(m), cols(i, k)])
-                    value = term if value is None else value + term
-                    value = value + rows_dot(turned(trace), matrix[1, span(m), cols(i, k)])
-                base[:, span(m)] += value
-
-        @pl.loop(0, blocks)
-        def _(k):
-            finish_down(k, base[:, span(k)])
+                base[:, span(m)] += down_term(m, [k])
+
+        wait_gather(blocks - 1)
+        for m in range(blocks):
+            finish_down(m, base[:, span(m)] + down_term(m, [blocks - 1]))
 
     def finish_up(k):
         value = acc[j, :, span(k)]
@@ -239,21 +261,28 @@
     def _():
         acc[...] = jnp.zeros_like(acc)
 
-        @pl.loop(0, blocks)
+        def up_term(trace, r, i, k):
+            value = cols_dot(trace, matrix[0, span(r), cols(i, k)])
+            return value + cols_dot(turned(trace), matrix[1, span(r), cols(i, k)])
+
+        @pl.loop(0, blocks - 1)
         def _(r):
             wait_up(r)
             trace = incoming[r]
             for i in range(peers):
                 for k in range(blocks):
-                    value = cols_dot(trace, matrix[0, span(r), cols(i, k)])
-                    value = value + cols_dot(turned(trace), matrix[1, span(r), cols(i, k)])
-                    acc[i, :, span(k)] += value
-
+                    acc[i, :, span(k)] += up_term(trace, r, i, k)
+
+        wait_up(blocks - 1)
+        last = incoming[blocks - 1]
         for d in range(1, peers):
             i = peer(d)
             for k in range(blocks):
-                part_out[i, k] = acc[i, :, span(k)].astype(BF16)
+                value = acc[i, :, span(k)] + up_term(last, blocks - 1, i, k)
+                part_out[i, k] = value.astype(BF16)
             share_all(d).start()
+        for k in range(blocks):
+            acc[j, :, span(k)] += up_term(last, blocks - 1, j, k)
         for d in range(1, peers):
             shared_all(d).wait_recv()
 

time: 95.5 us -> 90.6 us (0.949)
  Pallas kernels: 93.8 us -> 88.9 us
    pallas_call x1, Pallas kernels: 93.8 us -> 88.9 us  [local(): pl.pallas_call(functools.partial(sweeps, layers, peers, blocks), out_shap...]
where the time goes in v2:
time: 90.6 us; the launch traced here: 90.5 us
  Pallas kernels  88.9 us (98%)
  local copies, waits for them, and re-layouts  1.57 us (2%)
    pallas_call x1, Pallas kernels, local(): pl.pallas_call(functools.partial(sweeps, layers, peers, blocks), out_shap...  88.9 us

profile of v2, /device:TPU:1, one launch (start us, length us, event | category | flops | bytes accessed | tf_op | source)
XLA Modules:
  0.0 90.5 jit_solution(9804455752208697594)
XLA Ops:
  0.0 88.9 %shard_map.37 = f32[32,1024]{1,0:T(8,128)} custom-call(bf16[2,1024,8192]{2,1,0:T(8,128)(2,1)} %bitcast.4, f32[32,1024]{1,0:T(8,128)} %bitcast.6, f32[32,1024]{1,0:T(8,128)} %bitcast.7), custom_call_target="tpu_custom_call" | custom-call | tf_op jit(solution)/shard_map/pallas_call | solution.py:319
  88.9 1.6 %copy.5 = f32[1,2,16,1024]{3,2,1,0:T(8,128)} copy(f32[1,2,16,1024]{3,2,1,0:T(8,128)} %bitcast.5) | data formatting | bytes 262144
